TPU v7x, 32 devices: a whole 2x2x4 slice. The times are simulated.
32 devices in a mesh: wide: 16 (over z, y, x), narrow: 2 (over core).
Axes of the slice: x: 2, y: 2, z: 4, core: 2. Of those that a mesh axis runs over, the one named last changes fastest.
Arguments:
- cand_ids: int32 [32, 2048], P(None, ('wide', 'narrow')), may hold values from 0 to 59999
- cand_request: int32 [2048], P(('wide', 'narrow')), may hold values from 0 to 1
- tables: bfloat16 [32, 1024, 256], P('wide'), may hold values from -4 to 4
- table_rows: int32 [32], P('wide'), may hold values from 256 to 1024
- width_choice: int32 [32], P('wide'), may hold values from 0 to 3
- projections: bfloat16 [32, 256, 128], P('wide'), may hold values from -0.5 to 0.5
- user_dense: bfloat16 [32, 512], P(('wide', 'narrow')), may hold values from -6 to 6
- user_weight: bfloat16 [512, 1024], replicated, may hold values from -0.25 to 0.25
- cross_down: bfloat16 [2048, 256], P('narrow'), may hold values from -0.125 to 0.125
- cross_up: bfloat16 [256, 2048], P(None, 'narrow'), may hold values from -0.375 to 0.375
- cross_bias: float32 [2048], replicated, may hold values from -3 to 3
- deep_in: bfloat16 [2048, 512], P('narrow'), may hold values from -0.125 to 0.125
- deep_mid: bfloat16 [512, 256], replicated, may hold values from -0.25 to 0.25
- head_cross: float32 [2048], replicated, may hold values from -0.125 to 0.125
- head_deep: float32 [256], replicated, may hold values from -0.375 to 0.375
Outputs:
- crossed: bfloat16 [2048, 2048], P(('wide', 'narrow'))
- scores: float32 [2048], P(('wide', 'narrow'))
All inputs are finite; a program needn't handle non-finite values.
Results may differ from a plain program's by a relative error of at most 0.0072.
Values may be sent and summed in bfloat16 or wider, within the bound.
A program may use at most 64 MiB of HBM per device.

v0:
```python
import jax
import jax.numpy as jnp
from jax import lax
from jax.sharding import PartitionSpec as P

SLOTS = 8


def per_device(
    cand_ids,
    cand_request,
    tables,
    table_rows,
    width_choice,
    projections,
    user_dense,
    user_weight,
    cross_down,
    cross_up,
    cross_bias,
    deep_in,
    deep_mid,
    head_cross,
    head_deep,
):
    nwide = lax.axis_size("wide")
    tab_dev = tables.shape[0]
    emb_width = tables.shape[2]
    rows_dev = cand_request.shape[0]
    columns = jnp.arange(emb_width, dtype=jnp.int32)
    feature_ids = cand_ids.reshape(nwide, tab_dev, rows_dev)
    received = lax.all_to_all(feature_ids, "wide", split_axis=0, concat_axis=0, tiled=True)
    results = []
    for t in range(tab_dev):
        index = jnp.remainder(received[:, t, :], table_rows[t])
        looked = jnp.take(tables[t], index, axis=0)
        width = jnp.left_shift(jnp.int32(32), width_choice[t])
        looked = jnp.where(columns < width, looked, jnp.zeros((), jnp.bfloat16))
        results.append(
            jnp.einsum(
                "sie,ep->sip", looked, projections[t], preferred_element_type=jnp.float32
            ).astype(jnp.bfloat16)
        )
    stacked = jnp.stack(results, axis=1)
    pooled = jnp.sum(stacked, axis=1, keepdims=True, dtype=jnp.float32).astype(jnp.bfloat16)
    returned = lax.all_to_all(pooled, "wide", split_axis=0, concat_axis=0, tiled=True)
    owners = jnp.sum(returned, axis=1, dtype=jnp.float32).astype(jnp.bfloat16)
    slots = jnp.sum(
        owners.reshape(nwide // SLOTS, SLOTS, rows_dev, owners.shape[2]), axis=0, dtype=jnp.float32
    ).astype(jnp.bfloat16)
    item = slots.transpose(1, 0, 2).reshape(rows_dev, SLOTS * owners.shape[2])
    mine = jax.nn.silu(jnp.dot(user_dense, user_weight, preferred_element_type=jnp.float32)).astype(
        jnp.bfloat16
    )
    users = lax.all_gather(mine, "narrow", axis=0, tiled=True)
    req_count = users.shape[0]
    selector = (cand_request[:, None] == jnp.arange(req_count, dtype=jnp.int32)[None, :]).astype(
        jnp.bfloat16
    )
    user_part = jnp.dot(selector, users, preferred_element_type=jnp.float32).astype(jnp.bfloat16)
    x0 = jnp.concatenate([user_part, item], axis=1)
    low_sum = jnp.dot(
        x0,
        lax.all_gather(cross_down, "narrow", axis=0, tiled=True),
        preferred_element_type=jnp.float32,
    )
    deep_sum = jnp.dot(
        x0,
        lax.all_gather(deep_in, "narrow", axis=0, tiled=True),
        preferred_element_type=jnp.float32,
    )
    low = low_sum.astype(jnp.bfloat16)
    deep = jax.nn.relu(deep_sum).astype(jnp.bfloat16)
    upward = jnp.dot(
        low,
        lax.all_gather(cross_up, "narrow", axis=1, tiled=True),
        preferred_element_type=jnp.float32,
    )
    base = x0.astype(jnp.float32)
    crossed = (base * (upward + cross_bias) + base).astype(jnp.bfloat16)
    hidden = jax.nn.relu(jnp.dot(deep, deep_mid, preferred_element_type=jnp.float32))
    scores = jnp.dot(crossed.astype(jnp.float32), head_cross, precision=lax.Precision.HIGHEST)
    scores = scores + jnp.dot(hidden, head_deep, precision=lax.Precision.HIGHEST)
    return (crossed, scores)


def solution(mesh):
    return jax.shard_map(
        per_device,
        mesh=mesh,
        in_specs=(
            P(None, ("wide", "narrow")),
            P(("wide", "narrow")),
            P("wide", None, None),
            P("wide"),
            P("wide"),
            P("wide", None, None),
            P(("wide", "narrow"), None),
            P(),
            P("narrow", None),
            P(None, "narrow"),
            P(),
            P("narrow", None),
            P(),
            P(),
            P(),
        ),
        out_specs=(P(("wide", "narrow"), None), P(("wide", "narrow"))),
        check_vma=False,
    )
```

profile of v0, /device:TPU:0, one launch (start us, length us, event | category | flops | bytes accessed | tf_op | source)
XLA Modules:
  0.0 64.5 jit_solution(12365914392738426155)
XLA Ops:
  7.2 0.0 all-gather.5.cloned.1.call-start
  7.3 0.7 %all-gather.5.cloned.1.call-update = ((bf16[1024,256]{1,0:T(8,128)(2,1)}), bf16[2048,256]{1,0:T(8,128)(2,1)}) async-update(((), (), s32[]{:S(2)}) %all-gather.5.cloned.1.call-start, bf16[1024,256]{1,0:T(8,128)(2,1)} %param.25) | async-update | bytes 2097176
  7.9 0.0 all-gather.7.cloned.1.call-start
  8.0 0.7 %all-gather.7.cloned.1.call-update = ((bf16[256,1024]{1,0:T(8,128)(2,1)}), bf16[256,2048]{1,0:T(8,128)(2,1)}) async-update(((), (), s32[]{:S(2)}) %all-gather.7.cloned.1.call-start, bf16[256,1024]{1,0:T(8,128)(2,1)} %param.26) | async-update | bytes 2097176
  8.7 1.4 %reshape.93 = s32[16,1,128]{2,1,0:T(1,128)} reshape(s32[16,2,64]{2,1,0:T(2,128)} %bitcast.75) | data formatting | bytes 16384
  10.1 8.3 %all-to-all-start = ((s32[16,1,128]{2,1,0:T(1,128)}), s32[16,1,128]{2,1,0:T(1,128)S(1)}, u32[]{:S(2)}, u32[]{:S(2)}) async-start(s32[16,1,128]{2,1,0:T(1,128)} %reshape.93), calls=%async_computation | async-start | bytes 16384 | tf_op jit(solution)/shard_map/all_to_all | solution.py:32
  18.4 0.0 all-gather.9.cloned.1.call-start
  18.5 0.7 %all-gather.9.cloned.1.call-update = ((bf16[1024,512]{1,0:T(8,128)(2,1)}), bf16[2048,512]{1,0:T(8,128)(2,1)}) async-update(((), (), s32[]{:S(2)}) %all-gather.9.cloned.1.call-start, bf16[1024,512]{1,0:T(8,128)(2,1)} %param.28) | async-update | bytes 4194328
  19.2 0.6 fusion.36
  19.8 0.1 slice_bitcast_fusion.1
  19.9 0.6 %fusion.35 = (s32[1]{0:T(128)}, s32[1]{0:T(128)}) fusion(s32[2]{0:T(128)S(1)} %copy-done.7), kind=kLoop, calls=%fused_computation.66 | loop fusion | bytes 16 | tf_op jit(solution)/shard_map/slice | solution.py:37
  24.4 1.3 %all-to-all-done = s32[16,1,128]{2,1,0:T(1,128)S(1)} async-done(((s32[16,1,128]{2,1,0:T(1,128)}), s32[16,1,128]{2,1,0:T(1,128)S(1)}, u32[]{:S(2)}, u32[]{:S(2)}) %all-to-all-start) | async-done | bytes 8224 | tf_op jit(solution)/shard_map/all_to_all | solution.py:32
  25.7 0.5 broadcast.24
  26.2 0.7 %reduce.4 = s32[16,128]{1,0:T(8,128)S(1)} reduce(s32[16,1,128]{2,1,0:T(1,128)S(1)} %all-to-all-done, s32[]{:T(128)} %broadcast.24), dimensions={1}, to_apply=%all_to_all.6.reduce_sub_computation | reduce | bytes 16388 | tf_op jit(solution)/shard_map/all_to_all | solution.py:32
  26.9 0.1 reshape.94
  26.9 0.7 %fusion.34 = (s32[16,1,64]{2,1,0:T(1,128)S(1)}, s32[16,1,64]{2,1,0:T(1,128)S(1)}) fusion(s32[16,2,64]{2,1,0:T(2,128)S(1)} %reshape.94, s32[]{:T(128)S(6)} %select_n.32), kind=kLoop, calls=%fused_computation.65 | loop fusion | flops 1024 | bytes 16388 | tf_op jit(solution)/shard_map/slice | solution.py:35
  27.6 0.1 reshape.80
  27.7 0.1 compare_and_fusion.1
  27.8 0.1 reshape.76
  27.9 3.9 %gather_fusion.1 = bf16[1024,256]{1,0:T(8,128)(2,1)S(1)} fusion(bf16[1024,256]{1,0:T(8,128)(2,1)S(1)} %get-tuple-element.8, s32[1024]{0:T(1024)S(1)} %broadcast_clamp_fusion), kind=kCustom, calls=%fused_computation.1.clone | custom fusion | bytes 1052672 | tf_op jit(solution)/shard_map/jit(_take)/gather | solution.py:36
  31.9 3.9 %gather_fusion = bf16[1024,256]{1,0:T(8,128)(2,1)S(1)} fusion(bf16[1024,256]{1,0:T(8,128)(2,1)S(1)} %get-tuple-element.7, s32[1024]{0:T(1024)S(1)} %broadcast_clamp_fusion.1), kind=kCustom, calls=%fused_computation.clone | custom fusion | bytes 1052672 | tf_op jit(solution)/shard_map/jit(_take)/gather | solution.py:36
  35.8 0.4 convolution_convert_fusion
  36.2 1.1 %fusion.4 = bf16[16,1,64,128]{3,2,1,0:T(8,128)(2,1)} fusion(bf16[16,64,128]{2,1,0:T(8,128)(2,1)S(1)} %convolution_convert_fusion, bf16[16,64,256]{2,1,0:T(8,128)(2,1)S(1)} %bitcast.71, pred[16,64]{1,0:T(8,128)(4,1)S(1)} %get-tuple-element.3, pred[256]{0:T(512)(128)(4,1)S(1)} %iota_compare_fusion.3, bf16[2,256,128]{2,1,0:T(8,128)(2,1)S(1)} %copy-done.10), kind=kOutput, calls=%fused_computation.9 | convolution fusion | flops 67895296 | bytes 1116672 | tf_op jit(solution)/shard_map/sie,ep->sip/dot_general | solution.py:40
  37.3 5.6 %all-to-all-start.1 = ((bf16[16,1,64,128]{3,2,1,0:T(8,128)(2,1)}), bf16[16,1,64,128]{3,2,1,0:T(8,128)(2,1)S(1)}, u32[]{:S(2)}, u32[]{:S(2)}) async-start(bf16[16,1,64,128]{3,2,1,0:T(8,128)(2,1)} %fusion.4), calls=%async_computation.1 | async-start | bytes 524288 | tf_op jit(solution)/shard_map/all_to_all | solution.py:46
  42.9 0.2 fusion.23
  43.2 2.0 %all-gather = bf16[2048]{0:T(1024)(128)(2,1)S(1)} all-gather(bf16[1024]{0:T(1024)(128)(2,1)S(1)} %multiply_convert_fusion), channel_id=2, replica_groups=mesh['wide'=16,'narrow'=2] {'narrow'}, dimensions={0}, use_global_device_ids=true | all-gather | bytes 6144 | tf_op jit(solution)/shard_map/all_gather | solution.py:55
  45.2 0.2 convolution_convert_fusion.2
  45.4 6.8 %all-to-all-done.1 = bf16[16,1,64,128]{3,2,1,0:T(8,128)(2,1)S(1)} async-done(((bf16[16,1,64,128]{3,2,1,0:T(8,128)(2,1)}), bf16[16,1,64,128]{3,2,1,0:T(8,128)(2,1)S(1)}, u32[]{:S(2)}, u32[]{:S(2)}) %all-to-all-start.1) | async-done | bytes 262176 | tf_op jit(solution)/shard_map/all_to_all | solution.py:46
  52.3 2.3 %fusion.2 = bf16[64,2048]{1,0:T(8,128)(2,1)S(1)} fusion(bf16[256,2048]{1,0:T(8,128)(2,1)} %all-gather.7.cloned.1.call-done, bf16[2048,256]{1,0:T(8,128)(2,1)} %all-gather.5.cloned.1.call-done, f32[2048]{0:T(1024)S(1)} %copy-done.4, bf16[64,1024]{1,0:T(8,128)(2,1)S(1)} %copy_bitcast_fusion, bf16[64,1024]{1,0:T(8,128)(2,1)S(1)} %convolution_convert_fusion.2), kind=kOutput, calls=%fused_computation.5 | convolution fusion | flops 135806976 | bytes 2629632 | tf_op jit(solution)/shard_map/dot_general | solution.py:74
  54.7 0.3 convolution_bitcast_fusion.1
  55.0 2.2 %convolution_maximum_fusion.1 = f32[64,256]{1,0:T(8,128)S(1)} fusion(bf16[512,256]{1,0:T(8,128)(2,1)S(1)} %copy-done.2, bf16[2048,512]{1,0:T(8,128)(2,1)} %all-gather.9.cloned.1.call-done, bf16[64,1024]{1,0:T(8,128)(2,1)S(1)} %copy_bitcast_fusion, bf16[64,1024]{1,0:T(8,128)(2,1)S(1)} %convolution_convert_fusion.2), kind=kOutput, calls=%fused_computation.13 | convolution fusion | flops 151601152 | bytes 2686976 | tf_op jit(solution)/shard_map/dot_general | solution.py:81
  57.3 0.7 %fusion.6 = f32[64]{0:T(128)} fusion(f32[64]{0:T(128)S(1)} %convolution_bitcast_fusion.1, f32[64,256]{1,0:T(8,128)S(1)} %convolution_maximum_fusion.1, f32[256,1]{0,1:T(1,128)S(1)} %bitcast.76), kind=kOutput, calls=%fused_computation.16 | convolution fusion | flops 196672 | bytes 67072 | tf_op jit(solution)/shard_map/dot_general | solution.py:83
  (36 shorter events, 0.2 us)
Async XLA Ops:
  7.2 35.7 %copy-start = (bf16[512,1024]{1,0:T(8,128)(2,1)S(1)}, bf16[512,1024]{1,0:T(8,128)(2,1)}, u32[]{:S(2)}) copy-start(bf16[512,1024]{1,0:T(8,128)(2,1)} %param.24) | copy-start | bytes 3145732
  7.2 12.0 %copy-start.6 = (s32[2]{0:T(128)S(1)}, s32[2]{0:T(128)}, u32[]{:S(2)}) copy-start(s32[2]{0:T(128)} %param.20) | copy-start | bytes 28
  7.2 12.6 %copy-start.1 = (bf16[2,1024,256]{2,1,0:T(8,128)(2,1)S(1)}, bf16[2,1024,256]{2,1,0:T(8,128)(2,1)}, u32[]{:S(2)}) copy-start(bf16[2,1024,256]{2,1,0:T(8,128)(2,1)} %param.19) | copy-start | bytes 3145732
  7.2 12.7 %copy-start.7 = (s32[2]{0:T(128)S(1)}, s32[2]{0:T(128)}, u32[]{:S(2)}) copy-start(s32[2]{0:T(128)} %param.21) | copy-start | bytes 28
  7.2 45.1 %all-gather.5.cloned.1.call-start = ((), (), s32[]{:S(2)}) async-start(), calls=%async_computation.2 | async-start | bytes 1572864 | tf_op jit(solution)/shard_map/all_gather | solution.py:64
  7.9 44.4 %all-gather.7.cloned.1.call-start = ((), (), s32[]{:S(2)}) async-start(), calls=%async_computation.3 | async-start | bytes 1572864 | tf_op jit(solution)/shard_map/all_gather | solution.py:76
  10.1 15.6 %all-to-all-start = ((s32[16,1,128]{2,1,0:T(1,128)}), s32[16,1,128]{2,1,0:T(1,128)S(1)}, u32[]{:S(2)}, u32[]{:S(2)}) async-start(s32[16,1,128]{2,1,0:T(1,128)} %reshape.93), calls=%async_computation | async-start | bytes 16384 | tf_op jit(solution)/shard_map/all_to_all | solution.py:32
  18.4 36.6 %all-gather.9.cloned.1.call-start = ((), (), s32[]{:S(2)}) async-start(), calls=%async_computation.4 | async-start | bytes 3145728 | tf_op jit(solution)/shard_map/all_gather | solution.py:69
  31.9 4.0 %copy-start.10 = (bf16[2,256,128]{2,1,0:T(8,128)(2,1)S(1)}, bf16[2,256,128]{2,1,0:T(8,128)(2,1)}, u32[]{:S(2)}) copy-start(bf16[2,256,128]{2,1,0:T(8,128)(2,1)} %param.22) | copy-start | bytes 393220
  35.8 7.1 %copy-start.5 = (bf16[1,512]{1,0:T(2,128)(2,1)S(1)}, bf16[1,512]{1,0:T(2,128)(2,1)}, u32[]{:S(2)}) copy-start(bf16[1,512]{1,0:T(2,128)(2,1)} %param.23) | copy-start | bytes 3076
  36.2 9.0 %copy-start.9 = (s32[64]{0:T(128)S(1)}, s32[64]{0:T(128)}, u32[]{:S(2)}) copy-start(s32[64]{0:T(128)} %param.18) | copy-start | bytes 772
  36.2 16.1 %copy-start.4 = (f32[2048]{0:T(1024)S(1)}, f32[2048]{0:T(1024)}, u32[]{:S(2)}) copy-start(f32[2048]{0:T(1024)} %param.27) | copy-start | bytes 24580
  37.3 14.9 %all-to-all-start.1 = ((bf16[16,1,64,128]{3,2,1,0:T(8,128)(2,1)}), bf16[16,1,64,128]{3,2,1,0:T(8,128)(2,1)S(1)}, u32[]{:S(2)}, u32[]{:S(2)}) async-start(bf16[16,1,64,128]{3,2,1,0:T(8,128)(2,1)} %fusion.4), calls=%async_computation.1 | async-start | bytes 524288 | tf_op jit(solution)/shard_map/all_to_all | solution.py:46
  43.2 11.6 %copy-start.11 = (f32[2048]{0:T(1024)S(1)}, f32[2048]{0:T(1024)}, u32[]{:S(2)}) copy-start(f32[2048]{0:T(1024)} %param.30) | copy-start | bytes 24580
  43.2 11.9 %copy-start.2 = (bf16[512,256]{1,0:T(8,128)(2,1)S(1)}, bf16[512,256]{1,0:T(8,128)(2,1)}, u32[]{:S(2)}) copy-start(bf16[512,256]{1,0:T(8,128)(2,1)} %param.29) | copy-start | bytes 786436
  54.7 3.3 %copy-start.3 = (bf16[64,2048]{1,0:T(8,128)(2,1)}, bf16[64,2048]{1,0:T(8,128)(2,1)S(1)}, u32[]{:S(2)}) copy-start(bf16[64,2048]{1,0:T(8,128)(2,1)S(1)} %fusion.2) | copy-start | bytes 786436
  54.7 2.6 %copy-start.8 = (f32[256]{0:T(256)S(1)}, f32[256]{0:T(256)}, u32[]{:S(2)}) copy-start(f32[256]{0:T(256)} %param.31) | copy-start | bytes 3076
Sparse Core Ops, SparseCore 0:
  9.6 11.7 all-gather.4
  22.9 10.2 all-gather.6
  34.7 11.7 all-gather.8
where the time goes:
time: 65 us; the launch traced here: 64.5 us
  between operations  17.8 us (27%)
  starting transfers between devices  14.1 us (22%)
  local copies, waits for them, and re-layouts  11.4 us (18%)
  waiting for transfers between devices  10.2 us (16%)
  matrix products  7.45 us (11%)
  blocking collectives  1.97 us (3%)
  other arithmetic  1.53 us (2%)
    all_to_all x1, starting transfers between devices, per_device(): lax.all_to_all(feature_ids, 'wide', split_axis=0, concat_axis=0, tiled=True)  8.34 us
    gather x2, local copies, waits for them, and re-layouts, per_device(): looked = jnp.take(tables[t], index, axis=0)  7.88 us
    all_to_all x1, waiting for transfers between devices, per_device(): lax.all_to_all(pooled, 'wide', split_axis=0, concat_axis=0, tiled=True)  6.81 us
    all_to_all x1, starting transfers between devices, per_device(): lax.all_to_all(pooled, 'wide', split_axis=0, concat_axis=0, tiled=True)  5.59 us
    dot_general x1, matrix products, per_device(): jnp.dot(low, lax.all_gather(cross_up, 'narrow', axis=1, tiled=True), pref...  2.34 us
    dot_general x1, matrix products, per_device(): jnp.dot(deep, deep_mid, preferred_element_type=jnp.float32)  2.22 us
    unnamed x3, waiting for transfers between devices  2.06 us
    all_gather x1, blocking collectives, per_device(): users = lax.all_gather(mine, 'narrow', axis=0, tiled=True)  1.97 us
  transfers between devices with their start and end apart: 5, of which 2 were waited for; matrix products, arithmetic and copies ran while one was open for 27% of the time, Pallas kernels for 0%

commit v1 on v0

v1 whole, which is shorter than its diff:
```python
import functools

import jax
import jax.numpy as jnp
from jax import lax
from jax.experimental import pallas as pl
from jax.experimental.pallas import tpu as pltpu
from jax.sharding import PartitionSpec as P

GROUP = 4
F32 = jnp.float32
BF16 = jnp.bfloat16


def dot(a, b):
    return jnp.dot(a, b, preferred_element_type=F32)


def row_to_column(row, eye):
    return jnp.sum(jnp.where(eye, row, 0.0), axis=1, keepdims=True)


def kernel(
    nw,
    nn,
    ids_in,
    request_in,
    tables_in,
    rows_in,
    choice_in,
    proj_in,
    dense_in,
    user_weight_in,
    down_in,
    up_in,
    bias_in,
    deep_in,
    mid_in,
    head_cross_in,
    head_deep_in,
    crossed_out,
    scores_out,
    ids,
    request,
    tables,
    rows,
    choice,
    proj,
    dense,
    user_weight,
    down,
    up,
    bias,
    deep_w,
    mid,
    head_cross,
    head_deep,
    ids_send,
    ids_recv,
    projected,
    onehot,
    emb_send,
    emb_recv,
    x0,
    crossed,
    scores,
    local_sem,
    out_sem,
    ids_ssem,
    ids_rsem,
    emb_ssem,
    emb_rsem,
    nar_ssem,
    nar_rsem,
):
    me = lax.axis_index("wide")
    core = lax.axis_index("narrow")
    tab_dev, vocab, emb_width = tables.shape
    cand = request.shape[1]
    width = projected.shape[1]
    total = bias.shape[1]
    user_dim = user_weight.shape[1]
    req_dev = dense.shape[1]
    block = down.shape[1]
    column_block = up.shape[2]

    loads = {}
    for at, (name, source, target) in enumerate(
        (
            ("ids", ids_in, ids),
            ("proj", proj_in, proj),
            ("choice", choice_in, choice),
            ("rows", rows_in, rows),
            ("tables", tables_in, tables),
            ("dense", dense_in, dense.at[core]),
            ("request", request_in, request),
            ("user_weight", user_weight_in, user_weight),
            ("down", down_in, down.at[core]),
            ("deep", deep_in, deep_w.at[core]),
            ("up", up_in, up.at[core]),
            ("mid", mid_in, mid),
            ("bias", bias_in, bias),
            ("head_cross", head_cross_in, head_cross),
            ("head_deep", head_deep_in, head_deep),
        )
    ):
        loads[name] = pltpu.make_async_copy(source, target, local_sem.at[at])
        loads[name].start()

    barrier = pltpu.get_barrier_semaphore()

    def peer_of(j):
        return lax.rem(me + nw // 2 + (j // 2) * (1 - 2 * (j % 2)) - (j % 2) + nw, nw)

    def greet(j, carry):
        pl.semaphore_signal(
            barrier, inc=1, device_id={"wide": peer_of(j)}, device_id_type=pl.DeviceIdType.MESH
        )
        return carry

    lax.fori_loop(0, nw - 1, greet, 0, unroll=nw <= 16)
    for step in range(1, nn):
        pl.semaphore_signal(
            barrier,
            inc=1,
            device_id={"narrow": lax.rem(core + step, nn)},
            device_id_type=pl.DeviceIdType.MESH,
        )

    loads["ids"].wait()
    for o in range(nw):
        ids_send[o] = ids[o * tab_dev : (o + 1) * tab_dev, :]
    ids_recv[me] = ids_send[me]

    loads["proj"].wait()
    loads["choice"].wait()
    loads["tables"].wait()
    row_index = lax.broadcasted_iota(jnp.int32, (emb_width, width), 0)
    for t in range(tab_dev):
        kept = jnp.left_shift(jnp.full((1, 1), 32, jnp.int32), choice[:, t : t + 1])
        used = jnp.where(row_index < kept, proj[t].astype(F32), 0.0).astype(BF16)
        projected[t * vocab : (t + 1) * vocab, :] = dot(tables[t], used).astype(BF16)

    pl.semaphore_wait(barrier, nw - 1 + nn - 1)

    def ids_copy(to, index):
        return pltpu.make_async_remote_copy(
            src_ref=ids_send.at[to],
            dst_ref=ids_recv.at[index],
            send_sem=ids_ssem.at[to],
            recv_sem=ids_rsem.at[index],
            device_id={"wide": to},
            device_id_type=pl.DeviceIdType.MESH,
        )

    def emb_copy(to, index):
        return pltpu.make_async_remote_copy(
            src_ref=emb_send.at[to],
            dst_ref=emb_recv.at[index],
            send_sem=emb_ssem.at[to],
            recv_sem=emb_rsem.at[index],
            device_id={"wide": to},
            device_id_type=pl.DeviceIdType.MESH,
        )

    def narrow_copy(kind, to, index):
        source, target = (
            (dense_in, dense),
            (down_in, down),
            (deep_in, deep_w),
            (up_in, up),
        )[kind]
        return pltpu.make_async_remote_copy(
            src_ref=source,
            dst_ref=target.at[index],
            send_sem=nar_ssem.at[kind, to],
            recv_sem=nar_rsem.at[kind, index],
            device_id={"narrow": to},
            device_id_type=pl.DeviceIdType.MESH,
        )

    def send_ids(j, carry):
        ids_copy(peer_of(j), me).start()
        return carry

    lax.fori_loop(0, nw - 1, send_ids, 0, unroll=nw <= 16)
    for kind in range(4):
        for step in range(1, nn):
            narrow_copy(kind, lax.rem(core + step, nn), core).start()

    eye = lax.broadcasted_iota(jnp.int32, (cand, cand), 0) == lax.broadcasted_iota(
        jnp.int32, (cand, cand), 1
    )
    for name in ("request", "user_weight", "dense", "rows"):
        loads[name].wait()
    wanted = row_to_column(request[...].astype(F32), eye)
    for step in range(1, nn):
        narrow_copy(0, core, lax.rem(core + step, nn)).wait_recv()
    chosen = jnp.zeros((cand, dense.shape[2]), F32)
    for n in range(nn):
        for r in range(req_dev):
            chosen = jnp.where(
                wanted == float(n * req_dev + r), dense[n, r : r + 1, :].astype(F32), chosen
            )
    x0[:, :user_dim] = jax.nn.silu(dot(chosen.astype(BF16), user_weight[...])).astype(BF16)

    limit = rows[...].astype(F32)
    inverse = 1.0 / limit
    lane = lax.broadcasted_iota(jnp.int32, (cand, vocab), 1).astype(F32)

    def look_up(group, last):
        for i in range(GROUP):
            j = group * GROUP + i
            peer = peer_of(j)
            if not (last and i == GROUP - 1):
                ids_copy(me, peer).wait_recv()
            values = ids_recv[peer].astype(F32)
            for t in range(tab_dev):
                value = values[t : t + 1, :]
                most = limit[:, t : t + 1]
                index = value - jnp.floor(value * inverse[:, t : t + 1]) * most
                index = jnp.where(index < 0.0, index + most, index)
                index = jnp.where(index >= most, index - most, index)
                onehot[i * cand : (i + 1) * cand, t * vocab : (t + 1) * vocab] = jnp.where(
                    row_to_column(index, eye) == lane, 1.0, 0.0
                ).astype(BF16)
        pooled = dot(onehot[...], projected[...]).astype(BF16)
        for i in range(GROUP):
            j = group * GROUP + i
            part = pooled[i * cand : (i + 1) * cand]
            if last and i == GROUP - 1:
                emb_recv[me] = part
            else:
                peer = peer_of(j)
                emb_send[peer] = part
                emb_copy(peer, me).start()

    groups = nw // GROUP

    def look_up_loop(group, carry):
        look_up(group, False)
        return carry

    lax.fori_loop(0, groups - 1, look_up_loop, 0)
    look_up(groups - 1, True)

    for name in ("down", "deep"):
        loads[name].wait()
    for kind in (1, 2):
        for step in range(1, nn):
            narrow_copy(kind, core, lax.rem(core + step, nn)).wait_recv()
    low = jnp.zeros((cand, down.shape[2]), F32)
    deep = jnp.zeros((cand, deep_w.shape[2]), F32)
    for n in range(user_dim // block):
        part = x0[:, n * block : (n + 1) * block]
        low = low + dot(part, down[n])
        deep = deep + dot(part, deep_w[n])

    for name in ("up", "mid", "bias", "head_cross", "head_deep"):
        loads[name].wait()
    for step in range(1, nn):
        narrow_copy(3, core, lax.rem(core + step, nn)).wait_recv()

    def wait_emb(j, carry):
        emb_copy(me, peer_of(nw - 2 - j)).wait_recv()
        return carry

    lax.fori_loop(0, nw - 1, wait_emb, 0, unroll=nw <= 16)
    slots = (total - user_dim) // width
    for s in range(slots):
        item = emb_recv[s].astype(F32)
        for g in range(1, nw // slots):
            item = item + emb_recv[g * slots + s].astype(F32)
        x0[:, user_dim + s * width : user_dim + (s + 1) * width] = item.astype(BF16)
    for n in range(user_dim // block, total // block):
        part = x0[:, n * block : (n + 1) * block]
        low = low + dot(part, down[n])
        deep = deep + dot(part, deep_w[n])
    low = low.astype(BF16)
    deep = jax.nn.relu(deep).astype(BF16)
    score = jnp.zeros((cand, 1), F32)
    stores = []
    for n in range(nn):
        span = slice(n * column_block, (n + 1) * column_block)
        base = x0[:, span].astype(F32)
        out = (base * (dot(low, up[n]) + bias[:, span]) + base).astype(BF16)
        crossed[:, span] = out
        stores.append(pltpu.make_async_copy(crossed.at[:, span], crossed_out.at[:, span], out_sem.at[n]))
        stores[-1].start()
        score = score + jnp.sum(out.astype(F32) * head_cross[:, span], axis=1, keepdims=True)
    hidden = jax.nn.relu(dot(deep, mid[...]))
    score = score + jnp.sum(hidden * head_deep[...], axis=1, keepdims=True)
    scores[...] = jnp.sum(jnp.where(eye, score, 0.0), axis=0, keepdims=True)
    stores.append(pltpu.make_async_copy(scores, scores_out, out_sem.at[nn]))
    stores[-1].start()

    def drain(j, carry):
        ids_copy(peer_of(j), me).wait_send()
        emb_copy(peer_of(j), me).wait_send()
        return carry

    lax.fori_loop(0, nw - 1, drain, 0, unroll=nw <= 16)
    for kind in range(4):
        for step in range(1, nn):
            narrow_copy(kind, lax.rem(core + step, nn), core).wait_send()
    for store in stores:
        store.wait()


def per_device(
    cand_ids,
    cand_request,
    tables,
    table_rows,
    width_choice,
    projections,
    user_dense,
    user_weight,
    cross_down,
    cross_up,
    cross_bias,
    deep_in,
    deep_mid,
    head_cross,
    head_deep,
):
    nw = lax.axis_size("wide")
    nn = lax.axis_size("narrow")
    cand = cand_request.shape[0]
    tab_dev, vocab, emb_width = tables.shape
    width = projections.shape[2]
    total = cross_bias.shape[0]
    operands = (
        cand_ids,
        cand_request.reshape(1, -1),
        tables,
        table_rows.reshape(1, -1),
        width_choice.reshape(1, -1),
        projections,
        user_dense,
        user_weight,
        cross_down,
        cross_up,
        cross_bias.reshape(1, -1),
        deep_in,
        deep_mid,
        head_cross.reshape(1, -1),
        head_deep.reshape(1, -1),
    )
    gathered = (6, 8, 9, 11)
    scratch = [
        pltpu.VMEM(((nn,) if at in gathered else ()) + a.shape, a.dtype)
        for at, a in enumerate(operands)
    ]
    scratch += [
        pltpu.VMEM((nw, tab_dev, cand), jnp.int32),
        pltpu.VMEM((nw, tab_dev, cand), jnp.int32),
        pltpu.VMEM((tab_dev * vocab, width), BF16),
        pltpu.VMEM((GROUP * cand, tab_dev * vocab), BF16),
        pltpu.VMEM((nw, cand, width), BF16),
        pltpu.VMEM((nw, cand, width), BF16),
        pltpu.VMEM((cand, total), BF16),
        pltpu.VMEM((cand, total), BF16),
        pltpu.VMEM((1, cand), F32),
        pltpu.SemaphoreType.DMA((len(operands),)),
        pltpu.SemaphoreType.DMA((nn + 1,)),
        pltpu.SemaphoreType.DMA((nw,)),
        pltpu.SemaphoreType.DMA((nw,)),
        pltpu.SemaphoreType.DMA((nw,)),
        pltpu.SemaphoreType.DMA((nw,)),
        pltpu.SemaphoreType.DMA((4, nn)),
        pltpu.SemaphoreType.DMA((4, nn)),
    ]
    crossed, scores = pl.pallas_call(
        functools.partial(kernel, nw, nn),
        out_shape=(
            jax.ShapeDtypeStruct((cand, total), BF16),
            jax.ShapeDtypeStruct((1, cand), F32),
        ),
        in_specs=[pl.BlockSpec(memory_space=pl.ANY)] * len(operands),
        out_specs=(pl.BlockSpec(memory_space=pl.ANY), pl.BlockSpec(memory_space=pl.ANY)),
        scratch_shapes=scratch,
        compiler_params=pltpu.CompilerParams(
            collective_id=0, has_side_effects=True, vmem_limit_bytes=48 * 1024 * 1024
        ),
        name="score",
    )(*operands)
    return crossed, scores.reshape(cand)


def solution(mesh):
    return jax.shard_map(
        per_device,
        mesh=mesh,
        in_specs=(
            P(None, ("wide", "narrow")),
            P(("wide", "narrow")),
            P("wide", None, None),
            P("wide"),
            P("wide"),
            P("wide", None, None),
            P(("wide", "narrow"), None),
            P(),
            P("narrow", None),
            P(None, "narrow"),
            P(),
            P("narrow", None),
            P(),
            P(),
            P(),
        ),
        out_specs=(P(("wide", "narrow"), None), P(("wide", "narrow"))),
        check_vma=False,
    )
```

time: 65 us -> 34.9 us (0.54)
  Pallas kernels: 0 us -> 20.7 us
  between operations: 17.8 us -> 0.68 us
  starting transfers between devices: 14.1 us -> 0 us
  waiting for transfers between devices: 10.2 us -> 0 us
  matrix products: 7.45 us -> 0 us
  blocking collectives: 1.97 us -> 0 us
  other arithmetic: 1.53 us -> 0 us
  local copies, waits for them, and re-layouts: 11.4 us -> 12.9 us
    pallas_call x0 -> x1, Pallas kernels: none -> 20.7 us  [per_device(): pl.pallas_call(functools.partial(kernel, nw, nn), out_shape=(jax.ShapeDty...]
    all_to_all x2 -> x0, starting transfers between devices: 13.9 us -> none  [the longest x1 8.34 us: per_device(): lax.all_to_all(feature_ids, 'wide', split_axis=0, concat_axis=0, tiled=True)]
    unnamed x26 -> x32, local copies, waits for them, and re-layouts: 1.55 us -> 12.9 us
    all_to_all x2 -> x0, waiting for transfers between devices: 8.12 us -> none  [the longest x1 6.81 us: per_device(): lax.all_to_all(pooled, 'wide', split_axis=0, concat_axis=0, tiled=True)]
    gather x2 -> x0, local copies, waits for them, and re-layouts: 7.88 us -> none  [per_device(): looked = jnp.take(tables[t], index, axis=0)]
    dot_general x8 -> x0, matrix products: 7.45 us -> none  [the longest x1 2.34 us: per_device(): jnp.dot(low, lax.all_gather(cross_up, 'narrow', axis=1, tiled=True), pref...]
    unnamed x3 -> x0, waiting for transfers between devices: 2.06 us -> none
    all_gather x1 -> x0, blocking collectives: 1.97 us -> none  [per_device(): users = lax.all_gather(mine, 'narrow', axis=0, tiled=True)]
  transfers between devices with their start and end apart: 5 -> 0, of which waited for: 2 -> 0; matrix products, arithmetic and copies ran while one was open for 27% -> 0% of each run, Pallas kernels for 0% -> 0%
where the time goes in v1:
time: 34.9 us; the launch traced here: 34.3 us
  Pallas kernels  20.7 us (59%)
  local copies, waits for them, and re-layouts  12.9 us (37%)
  between operations  0.68 us (2%)
    pallas_call x1, Pallas kernels, per_device(): pl.pallas_call(functools.partial(kernel, nw, nn), out_shape=(jax.ShapeDty...  20.7 us
    unnamed x32, local copies, waits for them, and re-layouts  12.9 us

profile of v1, /device:TPU:0, one launch (start us, length us, event | category | flops | bytes accessed | tf_op | source)
XLA Modules:
  0.0 34.3 jit_solution(16968556462413946687)
XLA Ops:
  0.6 0.0 copy-start.8
  0.6 0.0 copy-start.10
  0.7 0.0 copy-start.11
  0.7 0.7 %copy-done.8 = f32[2048]{0:T(1024)S(1)} copy-done((f32[2048]{0:T(1024)S(1)}, f32[2048]{0:T(1024)}, u32[]{:S(2)}) %copy-start.8) | copy-done | bytes 8216
  1.3 0.0 copy-done.10
  1.3 0.0 copy-done.11
  1.3 0.0 copy-start
  1.4 1.2 %copy-done = bf16[2,1024,256]{2,1,0:T(8,128)(2,1)S(1)} copy-done((bf16[2,1024,256]{2,1,0:T(8,128)(2,1)S(1)}, bf16[2,1024,256]{2,1,0:T(8,128)(2,1)}, u32[]{:S(2)}) %copy-start) | copy-done | bytes 1048600
  2.6 0.0 copy-start.1
  2.6 1.2 %copy-done.1 = bf16[512,1024]{1,0:T(8,128)(2,1)S(1)} copy-done((bf16[512,1024]{1,0:T(8,128)(2,1)S(1)}, bf16[512,1024]{1,0:T(8,128)(2,1)}, u32[]{:S(2)}) %copy-start.1) | copy-done | bytes 1048600
  3.8 0.0 copy-start.2
  3.8 1.2 %copy-done.2 = bf16[1024,512]{1,0:T(8,128)(2,1)S(1)} copy-done((bf16[1024,512]{1,0:T(8,128)(2,1)S(1)}, bf16[1024,512]{1,0:T(8,128)(2,1)}, u32[]{:S(2)}) %copy-start.2) | copy-done | bytes 1048600
  5.0 0.0 copy-start.3
  5.0 1.0 %copy-done.3 = bf16[1024,256]{1,0:T(8,128)(2,1)S(1)} copy-done((bf16[1024,256]{1,0:T(8,128)(2,1)S(1)}, bf16[1024,256]{1,0:T(8,128)(2,1)}, u32[]{:S(2)}) %copy-start.3) | copy-done | bytes 524312
  6.1 0.0 copy-start.4
  6.1 1.0 %copy-done.4 = bf16[256,1024]{1,0:T(8,128)(2,1)S(1)} copy-done((bf16[256,1024]{1,0:T(8,128)(2,1)S(1)}, bf16[256,1024]{1,0:T(8,128)(2,1)}, u32[]{:S(2)}) %copy-start.4) | copy-done | bytes 524312
  7.1 0.0 copy-start.5
  7.1 0.9 %copy-done.5 = bf16[512,256]{1,0:T(8,128)(2,1)S(1)} copy-done((bf16[512,256]{1,0:T(8,128)(2,1)S(1)}, bf16[512,256]{1,0:T(8,128)(2,1)}, u32[]{:S(2)}) %copy-start.5) | copy-done | bytes 262168
  8.1 0.0 copy-start.6
  8.1 0.9 %copy-done.6 = bf16[2,256,128]{2,1,0:T(8,128)(2,1)S(1)} copy-done((bf16[2,256,128]{2,1,0:T(8,128)(2,1)S(1)}, bf16[2,256,128]{2,1,0:T(8,128)(2,1)}, u32[]{:S(2)}) %copy-start.6) | copy-done | bytes 131096
  9.0 0.0 copy-start.7
  9.0 0.7 %copy-done.7 = s32[32,64]{1,0:T(8,128)S(1)} copy-done((s32[32,64]{1,0:T(8,128)S(1)}, s32[32,64]{1,0:T(8,128)}, u32[]{:S(2)}) %copy-start.7) | copy-done | bytes 8216
  9.7 0.0 copy-start.9
  9.7 0.7 %copy-done.9 = f32[2048]{0:T(1024)S(1)} copy-done((f32[2048]{0:T(1024)S(1)}, f32[2048]{0:T(1024)}, u32[]{:S(2)}) %copy-start.9) | copy-done | bytes 8216
  10.4 0.0 copy-start.12
  10.4 0.7 %copy-done.12 = s32[64]{0:T(128)S(1)} copy-done((s32[64]{0:T(128)S(1)}, s32[64]{0:T(128)}, u32[]{:S(2)}) %copy-start.12) | copy-done | bytes 280
  11.0 0.0 copy-start.13
  11.0 0.7 %copy-done.13 = s32[2]{0:T(128)S(1)} copy-done((s32[2]{0:T(128)S(1)}, s32[2]{0:T(128)}, u32[]{:S(2)}) %copy-start.13) | copy-done | bytes 32
  11.7 0.7 %copy-done.14 = s32[2]{0:T(128)S(1)} copy-done((s32[2]{0:T(128)S(1)}, s32[2]{0:T(128)}, u32[]{:S(2)}) %copy-start.14) | copy-done | bytes 32
  12.3 20.7 %score.1 = (bf16[64,2048]{1,0:T(8,128)(2,1)S(1)}, f32[1,64]{1,0:T(1,128)S(1)}) custom-call(s32[32,64]{1,0:T(8,128)S(1)} %copy-done.7, s32[1,64]{1,0:T(1,128)S(1)} %bitcast.10, bf16[2,1024,256]{2,1,0:T(8,128)(2,1)S(1)} %copy-done, s32[1,2]{1,0:T(1,128)S(1)} %bitcast.11, s32[1,2]{1,0:T(1,128)S(1)} %bitcast.12, bf16[2,256,128]{2,1,0:T(8,128)(2,1)S(1)} %copy-done.6, ...), custom_call_target="tpu_custom_call" | custom-call | tf_op jit(solution)/shard_map/score/pallas_call | solution.py:374
  33.1 0.7 %copy.19 = bf16[64,2048]{1,0:T(8,128)(2,1)} copy(bf16[64,2048]{1,0:T(8,128)(2,1)S(1)} %get-tuple-element.8) | data formatting | bytes 524288
  33.8 0.5 %copy.20 = f32[64]{0:T(128)} copy(f32[64]{0:T(128)S(1)} %bitcast.13) | data formatting | bytes 512
  (1 shorter events, 0.0 us)
Async XLA Ops:
  0.6 0.7 %copy-start.8 = (f32[2048]{0:T(1024)S(1)}, f32[2048]{0:T(1024)}, u32[]{:S(2)}) copy-start(f32[2048]{0:T(1024)} %param.25) | copy-start | bytes 24580
  0.6 0.7 %copy-start.10 = (bf16[1,512]{1,0:T(2,128)(2,1)S(1)}, bf16[1,512]{1,0:T(2,128)(2,1)}, u32[]{:S(2)}) copy-start(bf16[1,512]{1,0:T(2,128)(2,1)} %dense_in.1) | copy-start | bytes 3076
  0.7 0.7 %copy-start.11 = (f32[256]{0:T(256)S(1)}, f32[256]{0:T(256)}, u32[]{:S(2)}) copy-start(f32[256]{0:T(256)} %param.29) | copy-start | bytes 3076
  1.3 1.2 %copy-start = (bf16[2,1024,256]{2,1,0:T(8,128)(2,1)S(1)}, bf16[2,1024,256]{2,1,0:T(8,128)(2,1)}, u32[]{:S(2)}) copy-start(bf16[2,1024,256]{2,1,0:T(8,128)(2,1)} %tables_in.1) | copy-start | bytes 3145732
  2.6 1.2 %copy-start.1 = (bf16[512,1024]{1,0:T(8,128)(2,1)S(1)}, bf16[512,1024]{1,0:T(8,128)(2,1)}, u32[]{:S(2)}) copy-start(bf16[512,1024]{1,0:T(8,128)(2,1)} %user_weight_in.1) | copy-start | bytes 3145732
  3.8 1.2 %copy-start.2 = (bf16[1024,512]{1,0:T(8,128)(2,1)S(1)}, bf16[1024,512]{1,0:T(8,128)(2,1)}, u32[]{:S(2)}) copy-start(bf16[1024,512]{1,0:T(8,128)(2,1)} %deep_in.1) | copy-start | bytes 3145732
  5.0 1.0 %copy-start.3 = (bf16[1024,256]{1,0:T(8,128)(2,1)S(1)}, bf16[1024,256]{1,0:T(8,128)(2,1)}, u32[]{:S(2)}) copy-start(bf16[1024,256]{1,0:T(8,128)(2,1)} %down_in.1) | copy-start | bytes 1572868
  6.1 1.0 %copy-start.4 = (bf16[256,1024]{1,0:T(8,128)(2,1)S(1)}, bf16[256,1024]{1,0:T(8,128)(2,1)}, u32[]{:S(2)}) copy-start(bf16[256,1024]{1,0:T(8,128)(2,1)} %up_in.1) | copy-start | bytes 1572868
  7.1 0.9 %copy-start.5 = (bf16[512,256]{1,0:T(8,128)(2,1)S(1)}, bf16[512,256]{1,0:T(8,128)(2,1)}, u32[]{:S(2)}) copy-start(bf16[512,256]{1,0:T(8,128)(2,1)} %mid_in.1) | copy-start | bytes 786436
  8.1 0.9 %copy-start.6 = (bf16[2,256,128]{2,1,0:T(8,128)(2,1)S(1)}, bf16[2,256,128]{2,1,0:T(8,128)(2,1)}, u32[]{:S(2)}) copy-start(bf16[2,256,128]{2,1,0:T(8,128)(2,1)} %proj_in.1) | copy-start | bytes 393220
  9.0 0.7 %copy-start.7 = (s32[32,64]{1,0:T(8,128)S(1)}, s32[32,64]{1,0:T(8,128)}, u32[]{:S(2)}) copy-start(s32[32,64]{1,0:T(8,128)} %ids_in.1) | copy-start | bytes 24580
  9.7 0.7 %copy-start.9 = (f32[2048]{0:T(1024)S(1)}, f32[2048]{0:T(1024)}, u32[]{:S(2)}) copy-start(f32[2048]{0:T(1024)} %param.28) | copy-start | bytes 24580
  10.4 0.7 %copy-start.12 = (s32[64]{0:T(128)S(1)}, s32[64]{0:T(128)}, u32[]{:S(2)}) copy-start(s32[64]{0:T(128)} %param.16) | copy-start | bytes 772
  11.0 0.7 %copy-start.13 = (s32[2]{0:T(128)S(1)}, s32[2]{0:T(128)}, u32[]{:S(2)}) copy-start(s32[2]{0:T(128)} %param.18) | copy-start | bytes 28
  11.7 0.7 %copy-start.14 = (s32[2]{0:T(128)S(1)}, s32[2]{0:T(128)}, u32[]{:S(2)}) copy-start(s32[2]{0:T(128)} %param.19) | copy-start | bytes 28

commit v2 on v1

--- a/solution.py
+++ b/solution.py
@@ -8,6 +8,8 @@
 from jax.sharding import PartitionSpec as P
 
 GROUP = 4
+SPLIT = 4
+PLANES = 4
 F32 = jnp.float32
 BF16 = jnp.bfloat16
 
@@ -77,7 +79,8 @@
     core = lax.axis_index("narrow")
     tab_dev, vocab, emb_width = tables.shape
     cand = request.shape[1]
-    width = projected.shape[1]
+    part_rows = projected.shape[1]
+    width = projected.shape[2] // SPLIT
     total = bias.shape[1]
     user_dim = user_weight.shape[1]
     req_dev = dense.shape[1]
@@ -109,16 +112,29 @@
 
     barrier = pltpu.get_barrier_semaphore()
 
-    def peer_of(j):
-        return lax.rem(me + nw // 2 + (j // 2) * (1 - 2 * (j % 2)) - (j % 2) + nw, nw)
-
-    def greet(j, carry):
+    plane_size = nw // PLANES
+    my_plane = me // plane_size
+    my_half = my_plane // 2
+    planes = (2 - my_half, 3 - 3 * my_half, my_half * 2 + 1 - my_plane % 2, my_plane)
+
+    def peer_at(order, i):
+        return planes[order] * plane_size + (me + i + 1) % plane_size
+
+    def each_peer(do):
+        for order in range(PLANES):
+
+            def step(i, carry, order=order):
+                do(peer_at(order, i))
+                return carry
+
+            lax.fori_loop(0, plane_size - (order == PLANES - 1), step, 0, unroll=nw <= 16)
+
+    def greet(peer):
         pl.semaphore_signal(
-            barrier, inc=1, device_id={"wide": peer_of(j)}, device_id_type=pl.DeviceIdType.MESH
-        )
-        return carry
-
-    lax.fori_loop(0, nw - 1, greet, 0, unroll=nw <= 16)
+            barrier, inc=1, device_id={"wide": peer}, device_id_type=pl.DeviceIdType.MESH
+        )
+
+    each_peer(greet)
     for step in range(1, nn):
         pl.semaphore_signal(
             barrier,
@@ -139,7 +155,10 @@
     for t in range(tab_dev):
         kept = jnp.left_shift(jnp.full((1, 1), 32, jnp.int32), choice[:, t : t + 1])
         used = jnp.where(row_index < kept, proj[t].astype(F32), 0.0).astype(BF16)
-        projected[t * vocab : (t + 1) * vocab, :] = dot(tables[t], used).astype(BF16)
+        for h in range(SPLIT):
+            projected[t, :, h * width : (h + 1) * width] = dot(
+                tables[t, h * part_rows : (h + 1) * part_rows, :], used
+            ).astype(BF16)
 
     pl.semaphore_wait(barrier, nw - 1 + nn - 1)
 
@@ -179,11 +198,7 @@
             device_id_type=pl.DeviceIdType.MESH,
         )
 
-    def send_ids(j, carry):
-        ids_copy(peer_of(j), me).start()
-        return carry
-
-    lax.fori_loop(0, nw - 1, send_ids, 0, unroll=nw <= 16)
+    each_peer(lambda peer: ids_copy(peer, me).start())
     for kind in range(4):
         for step in range(1, nn):
             narrow_copy(kind, lax.rem(core + step, nn), core).start()
@@ -206,12 +221,12 @@
 
     limit = rows[...].astype(F32)
     inverse = 1.0 / limit
-    lane = lax.broadcasted_iota(jnp.int32, (cand, vocab), 1).astype(F32)
-
-    def look_up(group, last):
+    lane = lax.broadcasted_iota(jnp.int32, (cand, part_rows), 1).astype(F32)
+
+    def look_up(order, group, last):
+        highs = []
         for i in range(GROUP):
-            j = group * GROUP + i
-            peer = peer_of(j)
+            peer = peer_at(order, group * GROUP + i)
             if not (last and i == GROUP - 1):
                 ids_copy(me, peer).wait_recv()
             values = ids_recv[peer].astype(F32)
@@ -221,28 +236,44 @@
                 index = value - jnp.floor(value * inverse[:, t : t + 1]) * most
                 index = jnp.where(index < 0.0, index + most, index)
                 index = jnp.where(index >= most, index - most, index)
-                onehot[i * cand : (i + 1) * cand, t * vocab : (t + 1) * vocab] = jnp.where(
-                    row_to_column(index, eye) == lane, 1.0, 0.0
+                high = sum(
+                    jnp.where(index >= float(h * part_rows), 1.0, 0.0) for h in range(1, SPLIT)
+                )
+                low_index = row_to_column(index - high * float(part_rows), eye)
+                highs.append(row_to_column(high, eye))
+                onehot[t, i * cand : (i + 1) * cand, :] = jnp.where(
+                    low_index == lane, 1.0, 0.0
                 ).astype(BF16)
-        pooled = dot(onehot[...], projected[...]).astype(BF16)
+        found = [dot(onehot[t], projected[t]) for t in range(tab_dev)]
         for i in range(GROUP):
-            j = group * GROUP + i
-            part = pooled[i * cand : (i + 1) * cand]
+            total_rows = jnp.zeros((cand, width), F32)
+            for t in range(tab_dev):
+                high = highs[i * tab_dev + t]
+                for h in range(SPLIT):
+                    piece = found[t][i * cand : (i + 1) * cand, h * width : (h + 1) * width]
+                    total_rows = total_rows + jnp.where(high == float(h), piece, 0.0)
+            part = total_rows.astype(BF16)
             if last and i == GROUP - 1:
                 emb_recv[me] = part
             else:
-                peer = peer_of(j)
+                peer = peer_at(order, group * GROUP + i)
                 emb_send[peer] = part
                 emb_copy(peer, me).start()
 
-    groups = nw // GROUP
-
-    def look_up_loop(group, carry):
-        look_up(group, False)
-        return carry
-
-    lax.fori_loop(0, groups - 1, look_up_loop, 0)
-    look_up(groups - 1, True)
+    groups = plane_size // GROUP
+    for order in range(PLANES):
+        final = order == PLANES - 1
+
+        def look_up_loop(group, carry, order=order):
+            look_up(order, group, False)
+            return carry
+
+        if groups - final > 1:
+            lax.fori_loop(0, groups - final, look_up_loop, 0)
+        elif groups - final == 1:
+            look_up(order, 0, False)
+        if final:
+            look_up(order, groups - 1, True)
 
     for name in ("down", "deep"):
         loads[name].wait()
@@ -261,11 +292,7 @@
     for step in range(1, nn):
         narrow_copy(3, core, lax.rem(core + step, nn)).wait_recv()
 
-    def wait_emb(j, carry):
-        emb_copy(me, peer_of(nw - 2 - j)).wait_recv()
-        return carry
-
-    lax.fori_loop(0, nw - 1, wait_emb, 0, unroll=nw <= 16)
+    each_peer(lambda peer: emb_copy(me, peer).wait_recv())
     slots = (total - user_dim) // width
     for s in range(slots):
         item = emb_recv[s].astype(F32)
@@ -294,12 +321,11 @@
     stores.append(pltpu.make_async_copy(scores, scores_out, out_sem.at[nn]))
     stores[-1].start()
 
-    def drain(j, carry):
-        ids_copy(peer_of(j), me).wait_send()
-        emb_copy(peer_of(j), me).wait_send()
-        return carry
-
-    lax.fori_loop(0, nw - 1, drain, 0, unroll=nw <= 16)
+    def drain(peer):
+        ids_copy(peer, me).wait_send()
+        emb_copy(peer, me).wait_send()
+
+    each_peer(drain)
     for kind in range(4):
         for step in range(1, nn):
             narrow_copy(kind, lax.rem(core + step, nn), core).wait_send()
@@ -355,8 +381,8 @@
     scratch += [
         pltpu.VMEM((nw, tab_dev, cand), jnp.int32),
         pltpu.VMEM((nw, tab_dev, cand), jnp.int32),
-        pltpu.VMEM((tab_dev * vocab, width), BF16),
-        pltpu.VMEM((GROUP * cand, tab_dev * vocab), BF16),
+        pltpu.VMEM((tab_dev, vocab // SPLIT, SPLIT * width), BF16),
+        pltpu.VMEM((tab_dev, GROUP * cand, vocab // SPLIT), BF16),
         pltpu.VMEM((nw, cand, width), BF16),
         pltpu.VMEM((nw, cand, width), BF16),
         pltpu.VMEM((cand, total), BF16),
@@ -381,7 +407,7 @@
         out_specs=(pl.BlockSpec(memory_space=pl.ANY), pl.BlockSpec(memory_space=pl.ANY)),
         scratch_shapes=scratch,
         compiler_params=pltpu.CompilerParams(
-            collective_id=0, has_side_effects=True, vmem_limit_bytes=48 * 1024 * 1024
+            collective_id=0, has_side_effects=True, vmem_limit_bytes=67043328
         ),
         name="score",
     )(*operands)

time: 34.9 us -> 23.4 us (0.67)
  local copies, waits for them, and re-layouts: 12.9 us -> 2.19 us
  Pallas kernels: 20.7 us -> 20.3 us
    unnamed x32 -> x4, local copies, waits for them, and re-layouts: 12.9 us -> 2.19 us
    pallas_call x1, Pallas kernels: 20.7 us -> 20.3 us  [per_device(): pl.pallas_call(functools.partial(kernel, nw, nn), out_shape=(jax.ShapeDty...]
where the time goes in v2:
time: 23.4 us; the launch traced here: 23.1 us
  Pallas kernels  20.3 us (87%)
  local copies, waits for them, and re-layouts  2.19 us (9%)
  between operations  0.65 us (3%)
    pallas_call x1, Pallas kernels, per_device(): pl.pallas_call(functools.partial(kernel, nw, nn), out_shape=(jax.ShapeDty...  20.3 us
    unnamed x4, local copies, waits for them, and re-layouts  2.19 us

profile of v2, /device:TPU:0, one launch (start us, length us, event | category | flops | bytes accessed | tf_op | source)
XLA Modules:
  0.0 23.1 jit_solution(541191034729901535)
XLA Ops:
  0.6 20.3 %score.1 = (bf16[64,2048]{1,0:T(8,128)(2,1)}, f32[1,64]{1,0:T(1,128)}) custom-call(s32[32,64]{1,0:T(8,128)} %ids_in.1, s32[1,64]{1,0:T(1,128)} %bitcast.10, bf16[2,1024,256]{2,1,0:T(8,128)(2,1)} %tables_in.1, s32[1,2]{1,0:T(1,128)} %bitcast.11, s32[1,2]{1,0:T(1,128)} %bitcast.12, bf16[2,256,128]{2,1,0:T(8,128)(2,1)} %proj_in.1, bf16[1,512]{1,0:T(2,128)(2,1)} %dense_in.1, ...), custom_call_target="tpu_custom_call" | custom-call | tf_op jit(solution)/shard_map/score/pallas_call | solution.py:400
  20.9 0.0 copy-start
  21.0 1.7 %copy.19 = bf16[64,2048]{1,0:T(8,128)(2,1)} copy(bf16[64,2048]{1,0:T(8,128)(2,1)} %get-tuple-element.8) | data formatting | bytes 524288
  22.6 0.0 copy-done
  22.6 0.5 %copy.20 = f32[64]{0:T(128)} copy(f32[64]{0:T(128)S(1)} %bitcast.13) | data formatting | bytes 512
Async XLA Ops:
  20.9 1.7 %copy-start = (f32[1,64]{1,0:T(1,128)S(1)}, f32[1,64]{1,0:T(1,128)}, u32[]{:S(2)}) copy-start(f32[1,64]{1,0:T(1,128)} %get-tuple-element.5) | copy-start | bytes 772

commit v3 on v2

--- a/solution.py
+++ b/solution.py
@@ -40,8 +40,8 @@
     mid_in,
     head_cross_in,
     head_deep_in,
-    crossed_out,
-    scores_out,
+    crossed,
+    scores,
     ids,
     request,
     tables,
@@ -64,10 +64,7 @@
     emb_send,
     emb_recv,
     x0,
-    crossed,
-    scores,
     local_sem,
-    out_sem,
     ids_ssem,
     ids_rsem,
     emb_ssem,
@@ -306,20 +303,15 @@
     low = low.astype(BF16)
     deep = jax.nn.relu(deep).astype(BF16)
     score = jnp.zeros((cand, 1), F32)
-    stores = []
     for n in range(nn):
         span = slice(n * column_block, (n + 1) * column_block)
         base = x0[:, span].astype(F32)
         out = (base * (dot(low, up[n]) + bias[:, span]) + base).astype(BF16)
         crossed[:, span] = out
-        stores.append(pltpu.make_async_copy(crossed.at[:, span], crossed_out.at[:, span], out_sem.at[n]))
-        stores[-1].start()
         score = score + jnp.sum(out.astype(F32) * head_cross[:, span], axis=1, keepdims=True)
     hidden = jax.nn.relu(dot(deep, mid[...]))
     score = score + jnp.sum(hidden * head_deep[...], axis=1, keepdims=True)
     scores[...] = jnp.sum(jnp.where(eye, score, 0.0), axis=0, keepdims=True)
-    stores.append(pltpu.make_async_copy(scores, scores_out, out_sem.at[nn]))
-    stores[-1].start()
 
     def drain(peer):
         ids_copy(peer, me).wait_send()
@@ -329,8 +321,6 @@
     for kind in range(4):
         for step in range(1, nn):
             narrow_copy(kind, lax.rem(core + step, nn), core).wait_send()
-    for store in stores:
-        store.wait()
 
 
 def per_device(
@@ -386,10 +376,7 @@
         pltpu.VMEM((nw, cand, width), BF16),
         pltpu.VMEM((nw, cand, width), BF16),
         pltpu.VMEM((cand, total), BF16),
-        pltpu.VMEM((cand, total), BF16),
-        pltpu.VMEM((1, cand), F32),
         pltpu.SemaphoreType.DMA((len(operands),)),
-        pltpu.SemaphoreType.DMA((nn + 1,)),
         pltpu.SemaphoreType.DMA((nw,)),
         pltpu.SemaphoreType.DMA((nw,)),
         pltpu.SemaphoreType.DMA((nw,)),
@@ -399,18 +386,15 @@
     ]
     crossed, scores = pl.pallas_call(
         functools.partial(kernel, nw, nn),
-        out_shape=(
-            jax.ShapeDtypeStruct((cand, total), BF16),
-            jax.ShapeDtypeStruct((1, cand), F32),
-        ),
+        out_shape=(pltpu.VMEM((cand, total), BF16), pltpu.VMEM((1, cand), F32)),
         in_specs=[pl.BlockSpec(memory_space=pl.ANY)] * len(operands),
-        out_specs=(pl.BlockSpec(memory_space=pl.ANY), pl.BlockSpec(memory_space=pl.ANY)),
+        out_specs=(pl.BlockSpec(memory_space=pltpu.VMEM), pl.BlockSpec(memory_space=pltpu.VMEM)),
         scratch_shapes=scratch,
         compiler_params=pltpu.CompilerParams(
-            collective_id=0, has_side_effects=True, vmem_limit_bytes=67043328
+            collective_id=0, has_side_effects=True, vmem_limit_bytes=32 * 1024 * 1024
         ),
         name="score",
-    )(*operands)
+    )(*[pltpu.with_memory_space_constraint(a, pltpu.HBM) for a in operands])
     return crossed, scores.reshape(cand)
 
 

time: 23.4 us -> 22 us (0.940)
  local copies, waits for them, and re-layouts: 2.19 us -> 1.22 us
  Pallas kernels: 20.3 us -> 19.8 us
    unnamed x4 -> x2, local copies, waits for them, and re-layouts: 2.19 us -> 1.22 us
    pallas_call x1, Pallas kernels: 20.3 us -> 19.8 us  [per_device(): pl.pallas_call(functools.partial(kernel, nw, nn), out_shape=(pltpu.VMEM((...]
where the time goes in v3:
time: 22 us; the launch traced here: 21.7 us
  Pallas kernels  19.8 us (90%)
  local copies, waits for them, and re-layouts  1.22 us (6%)
  between operations  0.64 us (3%)
    pallas_call x1, Pallas kernels, per_device(): pl.pallas_call(functools.partial(kernel, nw, nn), out_shape=(pltpu.VMEM((...  19.8 us
    unnamed x2, local copies, waits for them, and re-layouts  1.22 us

profile of v3, /device:TPU:0, one launch (start us, length us, event | category | flops | bytes accessed | tf_op | source)
XLA Modules:
  0.0 21.7 jit_solution(12643019779098488886)
XLA Ops:
  0.6 19.8 %score.1 = (bf16[64,2048]{1,0:T(8,128)(2,1)S(1)}, f32[1,64]{1,0:T(1,128)S(1)}) custom-call(s32[32,64]{1,0:T(8,128)} %ids_in.1, s32[1,64]{1,0:T(1,128)} %bitcast.11, bf16[2,1024,256]{2,1,0:T(8,128)(2,1)} %tables_in.1, s32[1,2]{1,0:T(1,128)} %bitcast.12, s32[1,2]{1,0:T(1,128)} %bitcast.13, bf16[2,256,128]{2,1,0:T(8,128)(2,1)} %proj_in.1, ...), custom_call_target="tpu_custom_call" | custom-call | tf_op jit(solution)/shard_map/score/pallas_call | solution.py:387
  20.5 0.7 %copy.19 = bf16[64,2048]{1,0:T(8,128)(2,1)} copy(bf16[64,2048]{1,0:T(8,128)(2,1)S(1)} %get-tuple-element.6) | data formatting | bytes 524288
  21.2 0.5 %copy.20 = f32[64]{0:T(128)} copy(f32[64]{0:T(128)S(1)} %bitcast.7) | data formatting | bytes 512
